TPU v7x, 256 devices: a whole 4x4x8 slice. The times are simulated.
256 devices in a mesh: dp: 64 (over x, z, y_hi), ctx: 4 (over y_lo, core).
Axes of the slice: x: 4, y: 4 (y_hi: 2, y_lo: 2; y = y_hi * 2 + y_lo), z: 8, core: 2. Of those that a mesh axis runs over, the one named last changes fastest.
Arguments:
- q_short: bfloat16 [49152, 1024], P('dp', 'ctx'), may hold values from -64 to 64
- k_short: bfloat16 [49152, 1024], P('dp', 'ctx'), may hold values from -8 to 8
- v_short: bfloat16 [49152, 1024], P('dp', 'ctx'), may hold values from -6 to 6
- dout_short: bfloat16 [49152, 1024], P('dp', 'ctx'), may hold values from -6 to 6
- doc_lengths: int32 [64, 8], replicated, may hold values from 1 to 256, as said below
- doc_dest: int32 [64, 8], replicated, may hold values from 0 to 63, as said below
- q_long: bfloat16 [64, 512, 1024], P('dp', 'ctx'), may hold values from -64 to 64
- k_long: bfloat16 [64, 512, 1024], P('dp', 'ctx'), may hold values from -8 to 8
- v_long: bfloat16 [64, 512, 1024], P('dp', 'ctx'), may hold values from -6 to 6
- dout_long: bfloat16 [64, 512, 1024], P('dp', 'ctx'), may hold values from -6 to 6
- block_order: int32 [8], replicated, may hold values from 0 to 7, each once
Outputs:
- out_short: bfloat16 [57344, 1024], P('dp', 'ctx')
- dq_short: bfloat16 [49152, 1024], P('dp', 'ctx')
- dk_short: bfloat16 [49152, 1024], P('dp', 'ctx')
- dv_short: bfloat16 [49152, 1024], P('dp', 'ctx')
- out_long: bfloat16 [64, 512, 1024], P('dp', 'ctx')
- dq_long: bfloat16 [64, 512, 1024], P('dp', 'ctx')
- dk_long: bfloat16 [64, 512, 1024], P('dp', 'ctx')
- dv_long: bfloat16 [64, 512, 1024], P('dp', 'ctx')
Inputs may be any that keep to these rules, and one draw needn't show every extreme that they name: `doc_lengths`: row r lists in order the lengths of the documents packed on rank r; each row sums to 768. `doc_dest`: entry [r, j] is r, except that in each pair of ranks r and r + 32 exactly one assigns its last document to the other; such a document has at most 128 tokens, and some has exactly 128. `block_order`: A permutation.
All inputs are finite; a program needn't handle non-finite values.
Results may differ from a plain program's by a relative error of at most 0.015.
Values may be sent and summed in bfloat16 or wider, within the bound.
A program may use at most 64 MiB of HBM per device.

v0:
```python
import jax
import jax.numpy as jnp
from jax import lax
from jax.sharding import PartitionSpec as P

HEAD_DIM = 128


NEG = -1e30


def shifted(value, axis, steps):
    count = lax.axis_size(axis)
    pairs = [(source, (source + steps) % count) for source in range(count)]
    return lax.ppermute(value, axis, pairs)


def sent_together(arrays, axis, dim, along):
    ends, at = ([], 0)
    for a in arrays[:-1]:
        at += a.shape[along]
        ends.append(at)
    both = jnp.concatenate(arrays, axis=along)
    return tuple(jnp.split(lax.all_gather(both, axis, axis=dim, tiled=True), ends, axis=along))


def cut_along(shard, dim, peers):
    before, after = (shard.shape[:dim], shard.shape[dim + 1 :])
    return jnp.moveaxis(shard.reshape(*before, peers, -1, *after), dim, 0)


def sent_and_summed(shard, axis, dim):
    pieces = cut_along(shard, dim, lax.axis_size(axis))
    arrived = lax.all_to_all(pieces, axis, split_axis=0, concat_axis=0, tiled=True)
    return arrived.sum(axis=0)


def dot_rows(left, right):
    return lax.dot_general(
        left, right, (((1,), (1,)), ((), ())), preferred_element_type=jnp.float32
    )


def dot_cols(left, right):
    return lax.dot_general(
        left, right, (((0,), (0,)), ((), ())), preferred_element_type=jnp.float32
    )


def column_of(array, head):
    return array[:, head * HEAD_DIM : (head + 1) * HEAD_DIM]


def attend_head(queries, keys, values, douts, mask, scale):
    scores = dot_rows(queries, keys) * scale
    scores = jnp.where(mask, scores, NEG)
    top = jnp.max(scores, axis=1, keepdims=True)
    lse = top + jnp.log(jnp.sum(jnp.exp(scores - top), axis=1, keepdims=True))
    probs = jnp.where(mask, jnp.exp(scores - lse), 0.0)
    weights = probs.astype(jnp.bfloat16)
    attended = jnp.dot(weights, values, preferred_element_type=jnp.float32).astype(jnp.bfloat16)
    dprobs = dot_rows(douts, values)
    delta = jnp.sum(douts.astype(jnp.float32) * attended.astype(jnp.float32), axis=1)
    score_grads = (probs * (dprobs - delta[:, None])).astype(jnp.bfloat16)
    grad_q = jnp.dot(score_grads, keys, preferred_element_type=jnp.float32) * scale
    return (attended, grad_q, score_grads, weights, lse[:, 0], delta)


def block_pass(queries, keys, values, douts, mask, scale):
    heads = queries.shape[1] // HEAD_DIM
    attended_list, query_list, key_list, value_list = ([], [], [], [])
    for head in range(heads):
        q_head = column_of(queries, head)
        d_head = column_of(douts, head)
        attended, grad_q, score_grads, weights, lse, delta = attend_head(
            q_head, column_of(keys, head), column_of(values, head), d_head, mask, scale
        )
        attended_list.append(attended)
        query_list.append(grad_q)
        key_list.append(dot_cols(score_grads, q_head) * scale)
        value_list.append(dot_cols(weights, d_head))
    join = lambda parts: jnp.concatenate(parts, axis=1)
    return (join(attended_list), join(query_list), join(key_list), join(value_list))


def band_attention(queries, keys, values, douts, doc_of, live, scale):
    token_count, width = queries.shape
    block = token_count // 3
    place = jnp.arange(token_count, dtype=jnp.int32)
    attended_parts = []
    query_parts = []
    grad_k = jnp.zeros((token_count, width), jnp.float32)
    grad_v = jnp.zeros((token_count, width), jnp.float32)
    for number in range(3):
        query_start = number * block
        query_end = query_start + block
        key_start = max(0, query_start - block)
        mask = doc_of[None, key_start:query_end] == doc_of[query_start:query_end, None]
        mask = mask & (place[None, key_start:query_end] <= place[query_start:query_end, None])
        mask = mask & live[query_start:query_end, None] & live[None, key_start:query_end]
        attended, grad_q, part_k, part_v = block_pass(
            queries[query_start:query_end],
            keys[key_start:query_end],
            values[key_start:query_end],
            douts[query_start:query_end],
            mask,
            scale,
        )
        attended_parts.append(attended)
        query_parts.append(grad_q)
        grad_k = grad_k.at[key_start:query_end].add(part_k)
        grad_v = grad_v.at[key_start:query_end].add(part_v)
    attended = jnp.concatenate(attended_parts, axis=0)
    grad_q = jnp.concatenate(query_parts, axis=0)
    return (
        attended,
        grad_q.astype(jnp.bfloat16),
        grad_k.astype(jnp.bfloat16),
        grad_v.astype(jnp.bfloat16),
    )


def front_align(block, count_in, rows, axis):
    padded = jnp.concatenate([block, jnp.zeros_like(block)], axis=axis)
    return lax.dynamic_slice_in_dim(padded, rows - count_in, rows, axis)


def positions(block_order, total, rows):
    half = rows // 2
    index = jnp.arange(total, dtype=jnp.int32)
    onehot = (
        (index // half)[:, None] == jnp.arange(block_order.shape[0], dtype=jnp.int32)[None, :]
    ).astype(jnp.int32)
    return jnp.sum(onehot * block_order[None, :], axis=1) * half + index % half


def shards(
    q_short,
    k_short,
    v_short,
    dout_short,
    doc_lengths,
    doc_dest,
    q_long,
    k_long,
    v_long,
    dout_long,
    block_order,
):
    scale = HEAD_DIM ** (-0.5)
    token_count, features = q_short.shape
    count = doc_lengths.shape[1]
    ranks = doc_lengths.shape[0]
    half = lax.axis_size("dp") // 2
    move_rows = token_count // 6
    rank = lax.axis_index("dp")
    partner = (rank + half) % ranks
    length_row = lax.dynamic_index_in_dim(doc_lengths, rank, 0, keepdims=False)
    dest_row = lax.dynamic_index_in_dim(doc_dest, rank, 0, keepdims=False)
    partner_lengths = lax.dynamic_index_in_dim(doc_lengths, partner, 0, keepdims=False)
    partner_dest = lax.dynamic_index_in_dim(doc_dest, partner, 0, keepdims=False)
    moves = dest_row[count - 1] != rank
    tail = length_row[count - 1]
    incoming = jnp.where(partner_dest[count - 1] != partner, partner_lengths[count - 1], 0)
    starts = jnp.cumsum(length_row) - length_row
    place = jnp.arange(token_count, dtype=jnp.int32)
    doc_of = jnp.sum((place[:, None] >= starts[None, :]).astype(jnp.int32), axis=1) - 1
    moved = moves & (place >= token_count - tail)
    tail_moved = moved[token_count - move_rows :]
    slots = jnp.arange(move_rows, dtype=jnp.int32)
    zero = jnp.zeros((), jnp.bfloat16)
    attended, grad_q, grad_k, grad_v = band_attention(
        q_short, k_short, v_short, dout_short, doc_of, jnp.ones((token_count,), bool), scale
    )
    outgoing = jnp.where(tail_moved[:, None], attended[token_count - move_rows :], zero)
    arrived = shifted(outgoing, "dp", half)
    received = front_align(arrived, incoming, move_rows, 0)
    received = jnp.where((slots < incoming)[:, None], received, zero)
    own = jnp.where(moved[:, None], zero, attended)
    out_short = jnp.concatenate([own, received], axis=0)
    dq_short = grad_q
    rows = q_long.shape[1]
    wide = q_long.shape[2]
    heads = wide // HEAD_DIM
    total = rows * lax.axis_size("ctx")
    place_all = positions(block_order, total, rows)
    place_own = lax.dynamic_slice_in_dim(place_all, lax.axis_index("ctx") * rows, rows)
    local_q = q_long[0]
    local_k = k_long[0]
    local_v = v_long[0]
    local_d = dout_long[0]
    own_mask = place_all[None, :] <= place_own[:, None]
    join = lambda parts: jnp.concatenate(parts, axis=1)
    all_k, all_v = sent_together((local_k, local_v), "ctx", 0, 1)
    attended_list, query_list, grad_list, weight_list = ([], [], [], [])
    for head in range(heads):
        attended, grad_q, score_grads, weights, lse, delta = attend_head(
            column_of(local_q, head),
            column_of(all_k, head),
            column_of(all_v, head),
            column_of(local_d, head),
            own_mask,
            scale,
        )
        attended_list.append(attended)
        query_list.append(grad_q)
        grad_list.append(score_grads)
        weight_list.append(weights)
    long_att = join(attended_list)
    long_q = join(query_list)
    key_parts = []
    value_parts = []
    for head in range(heads):
        grads_part = grad_list[head]
        weights_part = weight_list[head]
        key_parts.append(dot_cols(grads_part, column_of(local_q, head)) * scale)
        value_parts.append(dot_cols(weights_part, column_of(local_d, head)))
    summed = sent_and_summed(jnp.concatenate(key_parts + value_parts, axis=1), "ctx", 0)
    long_k = summed[:, :wide]
    long_v = summed[:, wide:]
    out_long = long_att.reshape(1, rows, wide)
    dq_long = long_q.astype(jnp.bfloat16).reshape(1, rows, wide)
    dk_long = long_k.astype(jnp.bfloat16).reshape(1, rows, wide)
    dv_long = long_v.astype(jnp.bfloat16).reshape(1, rows, wide)
    return (out_short, dq_short, grad_k, grad_v, out_long, dq_long, dk_long, dv_long)


def solution(mesh):
    placed = (
        P("dp", "ctx"),
        P("dp", "ctx"),
        P("dp", "ctx"),
        P("dp", "ctx"),
        P(),
        P(),
        P("dp", "ctx", None),
        P("dp", "ctx", None),
        P("dp", "ctx", None),
        P("dp", "ctx", None),
        P(),
    )
    return jax.shard_map(
        shards,
        mesh=mesh,
        in_specs=placed,
        out_specs=(
            P("dp", "ctx"),
            P("dp", "ctx"),
            P("dp", "ctx"),
            P("dp", "ctx"),
            P("dp", "ctx", None),
            P("dp", "ctx", None),
            P("dp", "ctx", None),
            P("dp", "ctx", None),
        ),
        check_vma=False,
    )
```

profile of v0, /device:TPU:1, one launch (start us, length us, event | category | flops | bytes accessed | tf_op | source)
XLA Modules:
  0.0 134.3 jit_solution(6430224031054870822)
XLA Ops:
  7.2 1.9 %pad_maximum_fusion = bf16[128,2048]{1,0:T(8,128)(2,1)} fusion(bf16[128,1024]{1,0:T(8,128)(2,1)} %bitcast.176, bf16[128,1024]{1,0:T(8,128)(2,1)} %bitcast.177), kind=kLoop, calls=%fused_computation.194 | loop fusion | flops 1048576 | bytes 1048576 | tf_op jit(solution)/shard_map/concatenate | solution.py:23
  9.3 1.4 %constant_dynamic-slice_fusion.2 = (s32[1,8]{0,1:T(8,128)S(1)}, s32[1,8]{0,1:T(8,128)S(1)}, s32[1,8]{0,1:T(8,128)}, s32[1,8]{0,1:T(8,128)S(1)}) fusion(s32[64,8]{0,1:T(8,128)} %param.27, s32[]{:T(128)S(6)} %select_n.143, s32[]{:T(128)S(6)} %select_n.158, s32[64,8]{0,1:T(8,128)} %param.28), kind=kLoop, calls=%fused_computation.380 | loop fusion | bytes 264 | tf_op jit(solution)/shard_map/jit(dynamic_index_in_dim)/dynamic_slice | solution.py:158
  11.6 1.3 fusion.266
  18.5 3.6 %collective-permute-start = (bf16[128,256]{0,1:T(8,128)(2,1)}, bf16[128,256]{0,1:T(8,128)(2,1)}, u32[]{:S(2)}, u32[]{:S(2)}) collective-permute-start(bf16[128,256]{0,1:T(8,128)(2,1)} %fusion.155), channel_id=1, source_target_pairs={{0,128},{4,132},{8,136},{12,140},{16,144},{20,148},{24,152},{28,15... | collective-permute-start | bytes 196616 | tf_op jit(solution)/shard_map/ppermute | solution.py:15
  26.5 1.9 %multiply_reduce_fusion.3 = (f32[256]{0:T(256)S(1)}, bf16[256,128]{0,1:T(8,128)(2,1)}) fusion(bf16[256,128]{0,1:T(8,128)(2,1)S(1)} %copy.141, bf16[768,256]{1,0:T(8,128)(2,1)} %param.25, f32[256,512]{1,0:T(8,128)S(1)} %get-tuple-element.136, f32[256]{0:T(256)S(1)} %log_add_fusion.3, s32[256]{0:T(256)S(1)} %slice.419, s32[512]{0:T(512)S(1)} %slice.418, ...), kind=kOutput, calls=%fused_computation.240 | convolution fusion | flops 34504448 | bytes 794624 | tf_op jit(solution)/shard_map/dot_general | solution.py:61
  28.4 1.2 fusion.11
  32.6 1.8 %multiply_reduce_fusion.5 = (f32[256]{0:T(256)S(1)}, bf16[256,128]{0,1:T(8,128)(2,1)}) fusion(bf16[256,128]{0,1:T(8,128)(2,1)S(1)} %copy.139, bf16[768,256]{1,0:T(8,128)(2,1)} %param.25, f32[256,256]{0,1:T(8,128)S(1)} %get-tuple-element.140, f32[256]{0:T(256)S(1)} %log_add_fusion.5, s32[256]{0:T(256)S(1)} %copy-done.55, s32[256]{0:T(256)S(1)} %copy-done.62), kind=kOutput, calls=%fused_computation.242 | convolution fusion | flops 17334016 | bytes 464896 | tf_op jit(solution)/shard_map/dot_general | solution.py:61
  34.4 1.0 fusion.56
  35.8 1.8 %multiply_reduce_fusion.4 = (f32[256]{0:T(256)S(1)}, bf16[256,128]{0,1:T(8,128)(2,1)}) fusion(bf16[256,128]{0,1:T(8,128)(2,1)S(1)} %copy.140, bf16[768,256]{1,0:T(8,128)(2,1)} %param.25, f32[256,256]{0,1:T(8,128)S(1)} %get-tuple-element.138, f32[256]{0:T(256)S(1)} %log_add_fusion.4, s32[256]{0:T(256)S(1)} %copy-done.56, s32[256]{0:T(256)S(1)} %copy-done.63), kind=kOutput, calls=%fused_computation.241 | convolution fusion | flops 17334016 | bytes 464896 | tf_op jit(solution)/shard_map/dot_general | solution.py:61
  37.6 1.0 fusion.57
  39.0 1.0 select_maximum_fusion
  40.9 1.5 %fusion.8 = bf16[256,512]{1,0:T(8,128)(2,1)S(1)} fusion(f32[256,512]{1,0:T(8,128)} %copy-done.5, f32[256]{0:T(256)S(1)} %copy-done.66, f32[256]{0:T(256)S(1)} %copy-done.45, bf16[768,256]{1,0:T(8,128)(2,1)} %param.25, bf16[768,256]{1,0:T(8,128)(2,1)} %param.26, s32[256]{0:T(256)S(1)} %copy-done.51, s32[512]{0:T(512)S(1)} %copy-done.35, ...), kind=kOutput, calls=%fused_computation.41 | convolution fusion | flops 34603008 | bytes 991232 | tf_op jit(solution)/shard_map/dot_general | solution.py:39
  42.5 1.1 convolution_multiply_fusion.20
  43.6 1.2 fusion.9
  44.9 1.1 convolution_multiply_fusion.21
  47.9 1.2 fusion.279
  49.3 1.2 fusion.278
  50.7 1.2 fusion.277
  52.1 1.3 fusion.276
  53.6 1.2 fusion.275
  55.0 1.2 fusion.274
  56.4 1.2 fusion.273
  57.8 1.2 fusion.272
  68.0 2.2 %copy_bitcast_fusion = f32[4,128,2048]{1,2,0:T(8,128)} fusion(f32[512,2048]{0,1:T(8,128)S(1)} %convolution_dynamic-update-slice_fusion), kind=kLoop, calls=%fused_computation | loop fusion | bytes 8388608 | tf_op jit(solution)/shard_map/reshape | solution.py:29
  70.2 5.7 %all-to-all-start = ((f32[4,128,2048]{1,2,0:T(8,128)}), f32[4,128,2048]{1,2,0:T(8,128)}, u32[]{:S(2)}, u32[]{:S(2)}) async-start(f32[4,128,2048]{1,2,0:T(8,128)} %copy_bitcast_fusion), calls=%async_computation | async-start | bytes 8388608 | tf_op jit(solution)/shard_map/all_to_all | solution.py:34
  76.2 1.2 slice.436
  82.6 1.0 maximum_select_fusion
  84.9 1.8 %copy.116 = bf16[1,128,1024]{2,1,0:T(8,128)(2,1)} copy(bf16[1,128,1024]{1,2,0:T(8,128)(2,1)} %bitcast.175) | data formatting | bytes 524288
  87.6 1.1 fusion.79
  88.8 1.1 fusion.77
  91.3 31.9 %all-to-all-done = f32[4,128,2048]{1,2,0:T(8,128)} async-done(((f32[4,128,2048]{1,2,0:T(8,128)}), f32[4,128,2048]{1,2,0:T(8,128)}, u32[]{:S(2)}, u32[]{:S(2)}) %all-to-all-start) | async-done | bytes 4194336 | tf_op jit(solution)/shard_map/all_to_all | solution.py:34
  123.2 2.5 %reduce_sum.309 = bf16[128,2048]{0,1:T(8,128)(2,1)S(1)} reduce(f32[4,128,2048]{1,2,0:T(8,128)} %all-to-all-done, f32[]{:T(128)} %constant.222.clone.1), dimensions={0}, to_apply=%region_45.46 | reduce | flops 786432 | bytes 4718596 | tf_op jit(solution)/shard_map/reduce_sum | solution.py:35
  (283 shorter events, 34.9 us)
Async XLA Ops:
  7.2 5.7 %copy-start = (bf16[768,256]{1,0:T(8,128)(2,1)S(1)}, bf16[768,256]{1,0:T(8,128)(2,1)}, u32[]{:S(2)}) copy-start(bf16[768,256]{1,0:T(8,128)(2,1)} %param.24) | copy-start | bytes 1179652
  7.2 5.7 %copy-start.21 = (bf16[768,256]{1,0:T(8,128)(2,1)S(1)}, bf16[768,256]{1,0:T(8,128)(2,1)}, u32[]{:S(2)}) copy-start(bf16[768,256]{1,0:T(8,128)(2,1)} %param.23) | copy-start | bytes 1179652
  7.2 7.9 %copy-start.22 = (bf16[768,256]{1,0:T(8,128)(2,1)S(1)}, bf16[768,256]{1,0:T(8,128)(2,1)}, u32[]{:S(2)}) copy-start(bf16[768,256]{1,0:T(8,128)(2,1)} %param.26) | copy-start | bytes 1179652
  7.2 40.7 %all-gather.2.cloned.1.call-start = ((), (), s32[]{:S(2)}) async-start(), calls=%async_computation.1 | async-start | bytes 2621440 | tf_op jit(solution)/shard_map/all_gather | solution.py:24
  9.3 7.6 %copy-start.50 = (s32[256]{0:T(256)}, s32[256]{0:T(256)S(1)}, u32[]{:S(2)}) copy-start(s32[256]{0:T(256)S(1)} %slice.429) | copy-start | bytes 3076
  9.3 7.6 %copy-start.34 = (s32[512]{0:T(512)}, s32[512]{0:T(512)S(1)}, u32[]{:S(2)}) copy-start(s32[512]{0:T(512)S(1)} %slice.428) | copy-start | bytes 6148
  11.5 5.4 %copy-start.57 = (s32[256]{0:T(256)}, s32[256]{0:T(256)S(1)}, u32[]{:S(2)}) copy-start(s32[256]{0:T(256)S(1)} %get-tuple-element.121) | copy-start | bytes 3076
  11.5 10.8 %copy-start.61 = (s32[256]{0:T(256)}, s32[256]{0:T(256)S(1)}, u32[]{:S(2)}) copy-start(s32[256]{0:T(256)S(1)} %get-tuple-element.120) | copy-start | bytes 3076
  11.5 16.9 %copy-start.59 = (s32[256]{0:T(256)}, s32[256]{0:T(256)S(1)}, u32[]{:S(2)}) copy-start(s32[256]{0:T(256)S(1)} %get-tuple-element.122) | copy-start | bytes 3076
  11.5 5.3 %copy-start.38 = (s32[512]{0:T(512)}, s32[512]{0:T(512)S(1)}, u32[]{:S(2)}) copy-start(s32[512]{0:T(512)S(1)} %get-tuple-element.124) | copy-start | bytes 6148
  11.6 16.9 %copy-start.40 = (s32[512]{0:T(512)}, s32[512]{0:T(512)S(1)}, u32[]{:S(2)}) copy-start(s32[512]{0:T(512)S(1)} %get-tuple-element.123) | copy-start | bytes 6148
  15.7 6.9 %copy-start.44 = (f32[256]{0:T(256)}, f32[256]{0:T(256)S(1)}, u32[]{:S(2)}) copy-start(f32[256]{0:T(256)S(1)} %log_add_fusion) | copy-start | bytes 3076
  15.9 6.8 %copy-start.42 = (f32[256]{0:T(256)}, f32[256]{0:T(256)S(1)}, u32[]{:S(2)}) copy-start(f32[256]{0:T(256)S(1)} %log_add_fusion.1) | copy-start | bytes 3076
  16.9 6.4 %copy-start.24 = (bf16[256,128]{0,1:T(8,128)(2,1)}, bf16[256,128]{0,1:T(8,128)(2,1)S(1)}, u32[]{:S(2)}) copy-start(bf16[256,128]{0,1:T(8,128)(2,1)S(1)} %get-tuple-element.142) | copy-start | bytes 196612
  17.8 6.5 %copy-start.26 = (bf16[256,128]{0,1:T(8,128)(2,1)}, bf16[256,128]{0,1:T(8,128)(2,1)S(1)}, u32[]{:S(2)}) copy-start(bf16[256,128]{0,1:T(8,128)(2,1)S(1)} %get-tuple-element.144) | copy-start | bytes 196612
  18.5 65.2 %collective-permute-start = (bf16[128,256]{0,1:T(8,128)(2,1)}, bf16[128,256]{0,1:T(8,128)(2,1)}, u32[]{:S(2)}, u32[]{:S(2)}) collective-permute-start(bf16[128,256]{0,1:T(8,128)(2,1)} %fusion.155), channel_id=1, source_target_pairs={{0,128},{4,132},{8,136},{12,140},{16,144},{20,148},{24,152},{28,15... | collective-permute-start | bytes 196616 | tf_op jit(solution)/shard_map/ppermute | solution.py:15
  22.1 6.4 %copy-start.52 = (s32[256]{0:T(256)}, s32[256]{0:T(256)S(1)}, u32[]{:S(2)}) copy-start(s32[256]{0:T(256)S(1)} %slice.419) | copy-start | bytes 3076
  22.1 6.4 %copy-start.36 = (s32[512]{0:T(512)}, s32[512]{0:T(512)S(1)}, u32[]{:S(2)}) copy-start(s32[512]{0:T(512)S(1)} %slice.418) | copy-start | bytes 6148
  35.8 5.1 %copy-start.35 = (s32[512]{0:T(512)S(1)}, s32[512]{0:T(512)}, u32[]{:S(2)}) copy-start(s32[512]{0:T(512)} %copy-done.34) | copy-start | bytes 6148
  35.8 5.1 %copy-start.39 = (s32[512]{0:T(512)S(1)}, s32[512]{0:T(512)}, u32[]{:S(2)}) copy-start(s32[512]{0:T(512)} %copy-done.38) | copy-start | bytes 6148
  35.8 5.1 %copy-start.45 = (f32[256]{0:T(256)S(1)}, f32[256]{0:T(256)}, u32[]{:S(2)}) copy-start(f32[256]{0:T(256)} %copy-done.44) | copy-start | bytes 3076
  35.8 5.1 %copy-start.51 = (s32[256]{0:T(256)S(1)}, s32[256]{0:T(256)}, u32[]{:S(2)}) copy-start(s32[256]{0:T(256)} %copy-done.50) | copy-start | bytes 3076
  35.8 5.1 %copy-start.58 = (s32[256]{0:T(256)S(1)}, s32[256]{0:T(256)}, u32[]{:S(2)}) copy-start(s32[256]{0:T(256)} %copy-done.57) | copy-start | bytes 3076
  35.8 5.1 %copy-start.66 = (f32[256]{0:T(256)S(1)}, f32[256]{0:T(256)}, u32[]{:S(2)}) copy-start(f32[256]{0:T(256)} %get-tuple-element.141) | copy-start | bytes 3076
  40.9 5.1 %copy-start.47 = (f32[256]{0:T(256)S(1)}, f32[256]{0:T(256)}, u32[]{:S(2)}) copy-start(f32[256]{0:T(256)} %copy-done.46) | copy-start | bytes 3076
  40.9 5.1 %copy-start.53 = (s32[256]{0:T(256)S(1)}, s32[256]{0:T(256)}, u32[]{:S(2)}) copy-start(s32[256]{0:T(256)} %copy-done.52) | copy-start | bytes 3076
  40.9 5.1 %copy-start.60 = (s32[256]{0:T(256)S(1)}, s32[256]{0:T(256)}, u32[]{:S(2)}) copy-start(s32[256]{0:T(256)} %copy-done.59) | copy-start | bytes 3076
  51.9 7.3 %copy-start.1 = (bf16[512,2048]{1,0:T(8,128)(2,1)S(1)}, bf16[512,2048]{1,0:T(8,128)(2,1)}, u32[]{:S(2)}) copy-start(bf16[512,2048]{1,0:T(8,128)(2,1)} %all-gather.2.cloned.1.call-done) | copy-start | bytes 6291460
  63.9 6.4 %copy-start.15 = (bf16[128,512]{1,0:T(8,128)(2,1)}, bf16[128,512]{1,0:T(8,128)(2,1)S(1)}, u32[]{:S(2)}) copy-start(bf16[128,512]{1,0:T(8,128)(2,1)S(1)} %fusion.52) | copy-start | bytes 393220
  70.2 53.0 %all-to-all-start = ((f32[4,128,2048]{1,2,0:T(8,128)}), f32[4,128,2048]{1,2,0:T(8,128)}, u32[]{:S(2)}, u32[]{:S(2)}) async-start(f32[4,128,2048]{1,2,0:T(8,128)} %copy_bitcast_fusion), calls=%async_computation | async-start | bytes 8388608 | tf_op jit(solution)/shard_map/all_to_all | solution.py:34
  83.9 6.1 %copy-start.18 = (bf16[128,512]{1,0:T(8,128)(2,1)S(1)}, bf16[128,512]{1,0:T(8,128)(2,1)}, u32[]{:S(2)}) copy-start(bf16[128,512]{1,0:T(8,128)(2,1)} %copy-done.17) | copy-start | bytes 393220
  83.9 6.3 %copy-start.20 = (bf16[128,512]{1,0:T(8,128)(2,1)S(1)}, bf16[128,512]{1,0:T(8,128)(2,1)}, u32[]{:S(2)}) copy-start(bf16[128,512]{1,0:T(8,128)(2,1)} %copy-done.19) | copy-start | bytes 393220
  (39 other events, 143.1 us)
Sparse Core Ops, SparseCore 0:
  9.8 35.8 all-gather.1
where the time goes:
time: 135 us; the launch traced here: 134 us
  matrix products  47.9 us (35%)
  waiting for transfers between devices  31.9 us (24%)
  between operations  18.2 us (13%)
  local copies, waits for them, and re-layouts  15.9 us (12%)
  other arithmetic  11 us (8%)
  starting transfers between devices  9.3 us (7%)
    all_to_all x1, waiting for transfers between devices, sent_and_summed(): lax.all_to_all(pieces, axis, split_axis=0, concat_axis=0, tiled=True)  31.9 us
    dot_general x28, matrix products, dot_rows(): lax.dot_general(left, right, (((1,), (1,)), ((), ())), preferred_element_...  20.5 us
    dot_general x14, matrix products, attend_head(): jnp.dot(weights, values, preferred_element_type=jnp.float32)  10.6 us
    dot_general x28, matrix products, dot_cols(): lax.dot_general(left, right, (((0,), (0,)), ((), ())), preferred_element_...  9.82 us
    unnamed x152, local copies, waits for them, and re-layouts  9.28 us
    dot_general x14, matrix products, attend_head(): jnp.dot(score_grads, keys, preferred_element_type=jnp.float32) * scale  6.98 us
    all_to_all x1, starting transfers between devices, sent_and_summed(): lax.all_to_all(pieces, axis, split_axis=0, concat_axis=0, tiled=True)  5.7 us
    ppermute x1, starting transfers between devices, shifted(): return lax.ppermute(value, axis, pairs)  3.56 us
  transfers between devices with their start and end apart: 3, of which 1 were waited for; matrix products, arithmetic and copies ran while one was open for 51% of the time, Pallas kernels for 0%

commit v1 on v0

v1 whole, which is shorter than its diff:
```python
import functools
import math

import jax
import jax.numpy as jnp
from jax import lax
from jax.experimental import pallas as pl
from jax.experimental.pallas import tpu as pltpu
from jax.sharding import PartitionSpec as P

D = 128
B = 128
NEG = -1e30
SCALE = D**-0.5
EXP_SCALE = SCALE * math.log2(math.e)
MESH = pl.DeviceIdType.MESH
BF16 = jnp.bfloat16
F32 = jnp.float32


def dot_nt(a, b):
    return lax.dot_general(a, b, (((1,), (1,)), ((), ())), preferred_element_type=F32)


def dot_tn(a, b):
    return lax.dot_general(a, b, (((0,), (0,)), ((), ())), preferred_element_type=F32)


def dot_nn(a, b):
    return lax.dot_general(a, b, (((1,), (0,)), ((), ())), preferred_element_type=F32)


def attend(q, k, v, do, mask):
    scores = mask(dot_nt(q, k))
    top = jnp.max(scores, axis=1, keepdims=True)
    e = jnp.exp2((scores - top) * EXP_SCALE)
    probs = e * (1.0 / jnp.sum(e, axis=1, keepdims=True))
    weights = probs.astype(BF16)
    attended = dot_nn(weights, v).astype(BF16)
    delta = jnp.sum(do.astype(F32) * attended.astype(F32), axis=1, keepdims=True)
    grads = (probs * (dot_nt(do, v) - delta)).astype(BF16)
    grad_q = (dot_nn(grads, k) * SCALE).astype(BF16)
    return attended, grad_q, weights, grads


def kernel(
    ranks,
    qs_hbm, ks_hbm, vs_hbm, ds_hbm, len_ref, dest_ref,
    ql_hbm, kl_hbm, vl_hbm, dl_hbm, order_ref,
    os_ref, dqs_ref, dks_ref, dvs_ref, ol_ref, dql_ref, dkl_ref, dvl_ref,
    short, arrived0, arrived1, placed, result, leaving, w_band, g_band, w_long, g_long, moved,
    short_sem, own_sem, in_send, in_recv, out_send, out_recv, move_send, move_recv,
):
    dp = lax.axis_index("dp")
    me = lax.axis_index("ctx")
    partner = lax.rem(dp + ranks // 2, ranks)
    peers = {2: lax.rem(me + 2, 4), 3: 3 - me, 1: me + 1 - 2 * lax.rem(me, 2)}
    tokens = qs_hbm.shape[0]
    heads = qs_hbm.shape[1] // D
    mine, half = ql_hbm.shape[1], ql_hbm.shape[2]
    rows = mine * half
    arrived = (arrived0, arrived1)
    halves = arrived0.shape[1]
    total = halves * half
    longs = (ql_hbm, kl_hbm, vl_hbm, dl_hbm)
    long_outs = (ol_ref, dql_ref, dkl_ref, dvl_ref)

    short_copies = [
        pltpu.make_async_copy(src, short.at[t], short_sem.at[t])
        for t, src in enumerate((qs_hbm, ks_hbm, vs_hbm, ds_hbm))
    ]
    own_copies = []
    for h in range(heads):
        for t in range(4):
            cols = pl.ds(pl.multiple_of(me * heads * D + h * D, D), D)
            own_copies.append(
                pltpu.make_async_copy(
                    longs[t].at[0, :, :, cols],
                    arrived[h].at[t, pl.ds(me * mine, mine), :, :],
                    own_sem.at[h, t],
                )
            )

    barrier = pltpu.get_barrier_semaphore()
    for peer in peers.values():
        pl.semaphore_signal(barrier, inc=1, device_id=(dp, peer), device_id_type=MESH)
    pl.semaphore_signal(barrier, inc=1, device_id=(partner, me), device_id_type=MESH)
    for copy in short_copies:
        copy.start()
    pl.semaphore_wait(barrier, 4)

    in_copies = {}
    for h in range(heads):
        for r, peer in peers.items():
            for t in range(4):
                cols = pl.ds(pl.multiple_of(peer * heads * D + h * D, D), D)
                copy = pltpu.make_async_remote_copy(
                    src_ref=longs[t].at[0, :, :, cols],
                    dst_ref=arrived[h].at[t, pl.ds(me * mine, mine), :, :],
                    send_sem=in_send.at[h, t, r - 1],
                    recv_sem=in_recv.at[h, t, r - 1],
                    device_id=(dp, peer),
                    device_id_type=MESH,
                )
                copy.start()
                in_copies[h, t, r] = copy
    for copy in own_copies:
        copy.start()
    for copy in short_copies:
        copy.wait()

    row = lax.broadcasted_iota(jnp.int32, (B, B), 0)
    col = lax.broadcasted_iota(jnp.int32, (B, B), 1)
    docs = len_ref.shape[0]
    lengths = [len_ref[j, dp] for j in range(docs)]
    tail = lengths[docs - 1]
    moves = dest_ref[docs - 1, dp] != dp
    tail_moved = jnp.where(moves, tail, 0)
    blocks = tokens // B

    def short_block(n):
        first = max(0, n - 2)
        start = jnp.zeros((B, B), jnp.int32)
        at = 0
        for j in range(docs - 1):
            at = at + lengths[j]
            start = jnp.where(row + n * B >= at, at, start)
        pieces = []
        for b in range(first, n + 1):
            piece = col + b * B >= start
            if b == n:
                piece = piece & (col <= row)
            pieces.append(piece)
        allowed = jnp.concatenate(pieces, axis=1) if len(pieces) > 1 else pieces[0]
        mask = lambda s: jnp.where(allowed, s, NEG)
        here = slice(n * B, (n + 1) * B)
        seen = slice(first * B, (n + 1) * B)
        outs = []
        for h in range(heads):
            c = slice(h * D, (h + 1) * D)
            attended, grad_q, weights, grads = attend(
                short[0, here, c], short[1, seen, c], short[2, seen, c], short[3, here, c], mask
            )
            dqs_ref[here, c] = grad_q
            for b in range(first, n + 1):
                to = slice((n - b) * B, (n - b + 1) * B)
                w_band[h, b, to, :] = weights[:, (b - first) * B : (b - first + 1) * B]
                g_band[h, b, to, :] = grads[:, (b - first) * B : (b - first + 1) * B]
            outs.append(attended)
        return here, jnp.concatenate(outs, axis=1)

    def short_keys(b):
        n = min(3, blocks - b) * B
        here = slice(b * B, (b + 1) * B)
        seen = slice(b * B, b * B + n)
        for h in range(heads):
            c = slice(h * D, (h + 1) * D)
            dks_ref[here, c] = (dot_tn(g_band[h, b, :n, :], short[0, seen, c]) * SCALE).astype(BF16)
            dvs_ref[here, c] = dot_tn(w_band[h, b, :n, :], short[3, seen, c]).astype(BF16)

    here, attended = short_block(blocks - 1)
    pick = (col == row + (B - tail_moved)) & (row < tail_moved)
    moved[...] = dot_nn(pick.astype(F32).astype(BF16), attended).astype(BF16)
    move = pltpu.make_async_remote_copy(
        src_ref=moved,
        dst_ref=os_ref.at[tokens : tokens + B, :],
        send_sem=move_send,
        recv_sem=move_recv,
        device_id=(partner, me),
        device_id_type=MESH,
    )
    move.start()
    keep = jnp.concatenate([row, row], axis=1) < B - tail_moved
    os_ref[here, :] = jnp.where(keep, attended.astype(F32), 0.0).astype(BF16)
    for n in range(blocks - 2, -1, -1):
        here, attended = short_block(n)
        os_ref[here, :] = attended
        short_keys(n + 1)
    short_keys(0)

    order = [order_ref[i] for i in range(halves)]
    found = []
    for p in range(halves):
        at = 0
        for i in range(halves):
            at = jnp.where(order[i] == p, i, at)
        found.append(at)
    lower = col <= row
    out_copies = []

    def store(t, n, value):
        for i in range(B // half):
            result[t, n * (B // half) + i] = value[i * half : (i + 1) * half]

    for h in range(heads):
        for t in range(4):
            own_copies[h * 4 + t].wait()
        for r in peers:
            for t in range(4):
                in_copies[h, t, r].wait_recv()
        for t in range(4):
            for p in range(halves):
                placed[t, p * half : (p + 1) * half, :] = arrived[h][t, found[p]]
        for n in range(total // B):
            here = slice(n * B, (n + 1) * B)
            seen = slice(0, (n + 1) * B)

            def mask(s):
                last = jnp.where(lower, s[:, n * B :], NEG)
                return jnp.concatenate([s[:, : n * B], last], axis=1) if n else last

            attended, grad_q, weights, grads = attend(
                placed[0, here, :], placed[1, seen, :], placed[2, seen, :], placed[3, here, :], mask
            )
            store(0, n, attended)
            store(1, n, grad_q)
            w_long[here, seen] = weights
            g_long[here, seen] = grads
        for b in range(total // B):
            here = slice(b * B, (b + 1) * B)
            rest = slice(b * B, total)
            store(2, b, (dot_tn(g_long[rest, here], placed[0, rest, :]) * SCALE).astype(BF16))
            store(3, b, dot_tn(w_long[rest, here], placed[3, rest, :]).astype(BF16))
        for t in range(4):
            for i in range(halves):
                leaving[h, t, i * half : (i + 1) * half, :] = result[t, order[i]]
        cols = pl.ds(pl.multiple_of(me * heads * D + h * D, D), D)
        for r, peer in peers.items():
            for t in range(4):
                copy = pltpu.make_async_remote_copy(
                    src_ref=leaving.at[h, t, pl.ds(pl.multiple_of(peer * rows, rows), rows), :],
                    dst_ref=long_outs[t].at[0, :, cols],
                    send_sem=out_send.at[h, t, r - 1],
                    recv_sem=out_recv.at[h, t, r - 1],
                    device_id=(dp, peer),
                    device_id_type=MESH,
                )
                copy.start()
                out_copies.append(copy)
        for t in range(4):
            long_outs[t][0, :, cols] = leaving[h, t, pl.ds(pl.multiple_of(me * rows, rows), rows), :]

    for copy in in_copies.values():
        copy.wait_send()
    move.wait()
    for copy in out_copies:
        copy.wait()


def settle(*refs):
    count = (len(refs) - 1) // 2
    copies = [
        pltpu.make_async_copy(refs[i], refs[count + i], refs[-1].at[i]) for i in range(count)
    ]
    for copy in copies:
        copy.start()
    for copy in copies:
        copy.wait()


def shards(*args):
    q_short, q_long = args[0], args[6]
    halves = args[10].shape[0]
    tokens, width = q_short.shape
    heads = width // D
    _, rows, wide = q_long.shape
    ctx = lax.axis_size("ctx")
    total = rows * ctx
    blocks = tokens // B
    cut = [a.reshape(1, halves // ctx, total // halves, wide) for a in args[6:10]]
    args = args[:4] + (args[4].T, args[5].T, *cut, args[10])
    vmem = pl.BlockSpec(memory_space=pltpu.VMEM)
    smem = pl.BlockSpec(memory_space=pltpu.SMEM)
    hbm = pl.BlockSpec(memory_space=pl.ANY)
    dma = pltpu.SemaphoreType.DMA
    shapes = [(tokens + B, width)] + [(tokens, width)] * 3 + [(1, rows, wide)] * 4
    outs = pl.pallas_call(
        functools.partial(kernel, lax.axis_size("dp")),
        out_shape=tuple(pltpu.VMEM(s, BF16) for s in shapes),
        in_specs=[hbm] * 4 + [smem] * 2 + [hbm] * 4 + [smem],
        out_specs=(vmem,) * 8,
        scratch_shapes=[
            pltpu.VMEM((4, tokens, width), BF16),
            pltpu.VMEM((4, halves, total // halves, D), BF16),
            pltpu.VMEM((4, halves, total // halves, D), BF16),
            pltpu.VMEM((4, total, D), BF16),
            pltpu.VMEM((4, halves, total // halves, D), BF16),
            pltpu.VMEM((heads, 4, total, D), BF16),
            pltpu.VMEM((heads, blocks, 3 * B, B), BF16),
            pltpu.VMEM((heads, blocks, 3 * B, B), BF16),
            pltpu.VMEM((total, total), BF16),
            pltpu.VMEM((total, total), BF16),
            pltpu.VMEM((B, width), BF16),
            dma((4,)),
            dma((heads, 4)),
            dma((heads, 4, 3)),
            dma((heads, 4, 3)),
            dma((heads, 4, 3)),
            dma((heads, 4, 3)),
            dma,
            dma,
        ],
        compiler_params=pltpu.CompilerParams(collective_id=0, has_side_effects=True),
        name="attention",
    )(*args)
    return pl.pallas_call(
        settle,
        out_shape=tuple(jax.ShapeDtypeStruct(s, BF16) for s in shapes),
        in_specs=[vmem] * 8,
        out_specs=(hbm,) * 8,
        scratch_shapes=[dma((8,))],
        name="settle",
    )(*[pltpu.with_memory_space_constraint(o, pltpu.VMEM) for o in outs])


def solution(mesh):
    short = P("dp", "ctx")
    long = P("dp", "ctx", None)
    return jax.shard_map(
        shards,
        mesh=mesh,
        in_specs=(short,) * 4 + (P(), P()) + (long,) * 4 + (P(),),
        out_specs=(short,) * 4 + (long,) * 4,
        check_vma=False,
    )
```

time: 135 us -> 32.8 us (0.24)
  matrix products: 47.9 us -> 0 us
  Pallas kernels: 0 us -> 32 us
  waiting for transfers between devices: 31.9 us -> 0 us
  between operations: 18.2 us -> 0.65 us
  local copies, waits for them, and re-layouts: 15.9 us -> 0 us
  other arithmetic: 11 us -> 0 us
  starting transfers between devices: 9.3 us -> 0 us
    dot_general x84 -> x0, matrix products: 47.9 us -> none  [the longest x28 20.5 us: dot_rows(): lax.dot_general(left, right, (((1,), (1,)), ((), ())), preferred_element_...]
    pallas_call x0 -> x2, Pallas kernels: none -> 32 us  [the longest x1 30.5 us: shards(): pl.pallas_call(functools.partial(kernel, lax.axis_size('dp')), out_shape=...]
    all_to_all x1 -> x0, waiting for transfers between devices: 31.9 us -> none  [sent_and_summed(): lax.all_to_all(pieces, axis, split_axis=0, concat_axis=0, tiled=True)]
    unnamed x152 -> x0, local copies, waits for them, and re-layouts: 9.28 us -> none
    all_to_all x1 -> x0, starting transfers between devices: 5.7 us -> none  [sent_and_summed(): lax.all_to_all(pieces, axis, split_axis=0, concat_axis=0, tiled=True)]
    reduce_sum x18 -> x0, other arithmetic: 5.31 us -> none  [the longest x14 2.6 us: attend_head(): lse = top + jnp.log(jnp.sum(jnp.exp(scores - top), axis=1, keepdims=True))]
    ppermute x1 -> x0, starting transfers between devices: 3.56 us -> none  [shifted(): return lax.ppermute(value, axis, pairs)]
    concatenate x5 -> x0, other arithmetic: 3.09 us -> none  [the longest x1 1.94 us: sent_together(): both = jnp.concatenate(arrays, axis=along)]
  transfers between devices with their start and end apart: 3 -> 0, of which waited for: 1 -> 0; matrix products, arithmetic and copies ran while one was open for 51% -> 0% of each run, Pallas kernels for 0% -> 0%
where the time goes in v1:
time: 32.8 us; the launch traced here: 32.7 us
  Pallas kernels  32 us (98%)
  between operations  0.65 us (2%)
    pallas_call x1, Pallas kernels, shards(): pl.pallas_call(functools.partial(kernel, lax.axis_size('dp')), out_shape=...  30.5 us
    pallas_call x1, Pallas kernels, shards(): pl.pallas_call(settle, out_shape=tuple((jax.ShapeDtypeStruct(s, BF16) for...  1.57 us

profile of v1, /device:TPU:1, one launch (start us, length us, event | category | flops | bytes accessed | tf_op | source)
XLA Modules:
  0.0 32.7 jit_solution(2007307992121760041)
XLA Ops:
  0.6 30.5 %attention.1 = (bf16[896,256]{1,0:T(8,128)(2,1)S(1)}, bf16[768,256]{1,0:T(8,128)(2,1)S(1)}, bf16[768,256]{1,0:T(8,128)(2,1)S(1)}, bf16[768,256]{1,0:T(8,128)(2,1...) custom-call(bf16[768,256]{1,0:T(8,128)(2,1)} %qs_hbm.1, ...), custom_call_target="tpu_custom_call" | custom-call | tf_op jit(solution)/shard_map/attention/pallas_call | solution.py:277
  31.1 1.6 %settle.1 = (bf16[896,256]{1,0:T(8,128)(2,1)}, bf16[768,256]{1,0:T(8,128)(2,1)}, bf16[768,256]{1,0:T(8,128)(2,1)}, bf16[768,256]{1,0:T(8,128)(2,1)}, bf16[1,128,...) custom-call(bf16[896,256]{1,0:T(8,128)(2,1)S(1)} %get-tuple-element., ...), custom_call_target="tpu_custom_call" | custom-call | tf_op jit(solution)/shard_map/settle/pallas_call | solution.py:306

commit v2 on v1

--- a/solution.py
+++ b/solution.py
@@ -45,11 +45,11 @@
 
 def kernel(
     ranks,
-    qs_hbm, ks_hbm, vs_hbm, ds_hbm, len_ref, dest_ref,
-    ql_hbm, kl_hbm, vl_hbm, dl_hbm, order_ref,
+    qs_hbm, ks_hbm, vs_hbm, ds_hbm, len_hbm, dest_hbm,
+    ql_hbm, kl_hbm, vl_hbm, dl_hbm, order_hbm,
     os_ref, dqs_ref, dks_ref, dvs_ref, ol_ref, dql_ref, dkl_ref, dvl_ref,
-    short, arrived0, arrived1, placed, result, leaving, w_band, g_band, w_long, g_long, moved,
-    short_sem, own_sem, in_send, in_recv, out_send, out_recv, move_send, move_recv,
+    len_ref, dest_ref, order_ref, staged, short, arrived0, arrived1, placed, result, leaving, w_band, g_band, w_long, g_long, moved,
+    int_sem, stage_sem, short_sem, own_sem, in_send, in_recv, out_send, out_recv, move_send, move_recv,
 ):
     dp = lax.axis_index("dp")
     me = lax.axis_index("ctx")
@@ -65,6 +65,15 @@
     longs = (ql_hbm, kl_hbm, vl_hbm, dl_hbm)
     long_outs = (ol_ref, dql_ref, dkl_ref, dvl_ref)
 
+    int_copies = [
+        pltpu.make_async_copy(src, dst, int_sem.at[i])
+        for i, (src, dst) in enumerate(
+            ((len_hbm, len_ref), (dest_hbm, dest_ref), (order_hbm, order_ref))
+        )
+    ]
+    stage_copies = [
+        pltpu.make_async_copy(longs[t], staged.at[t], stage_sem.at[t]) for t in range(4)
+    ]
     short_copies = [
         pltpu.make_async_copy(src, short.at[t], short_sem.at[t])
         for t, src in enumerate((qs_hbm, ks_hbm, vs_hbm, ds_hbm))
@@ -85,8 +94,10 @@
     for peer in peers.values():
         pl.semaphore_signal(barrier, inc=1, device_id=(dp, peer), device_id_type=MESH)
     pl.semaphore_signal(barrier, inc=1, device_id=(partner, me), device_id_type=MESH)
-    for copy in short_copies:
+    for copy in stage_copies + int_copies + own_copies + short_copies:
         copy.start()
+    for copy in stage_copies:
+        copy.wait()
     pl.semaphore_wait(barrier, 4)
 
     in_copies = {}
@@ -95,7 +106,7 @@
             for t in range(4):
                 cols = pl.ds(pl.multiple_of(peer * heads * D + h * D, D), D)
                 copy = pltpu.make_async_remote_copy(
-                    src_ref=longs[t].at[0, :, :, cols],
+                    src_ref=staged.at[t, 0, :, :, cols],
                     dst_ref=arrived[h].at[t, pl.ds(me * mine, mine), :, :],
                     send_sem=in_send.at[h, t, r - 1],
                     recv_sem=in_recv.at[h, t, r - 1],
@@ -104,9 +115,7 @@
                 )
                 copy.start()
                 in_copies[h, t, r] = copy
-    for copy in own_copies:
-        copy.start()
-    for copy in short_copies:
+    for copy in int_copies + short_copies:
         copy.wait()
 
     row = lax.broadcasted_iota(jnp.int32, (B, B), 0)
@@ -186,7 +195,7 @@
             at = jnp.where(order[i] == p, i, at)
         found.append(at)
     lower = col <= row
-    out_copies = []
+    out_copies = {}
 
     def store(t, n, value):
         for i in range(B // half):
@@ -236,15 +245,21 @@
                     device_id_type=MESH,
                 )
                 copy.start()
-                out_copies.append(copy)
+                out_copies[h, t, r] = copy
         for t in range(4):
             long_outs[t][0, :, cols] = leaving[h, t, pl.ds(pl.multiple_of(me * rows, rows), rows), :]
 
     for copy in in_copies.values():
         copy.wait_send()
     move.wait()
-    for copy in out_copies:
-        copy.wait()
+    for r in (1, 2, 3):
+        for h in range(heads):
+            for t in range(4):
+                out_copies[h, t, r].wait_send()
+    for r in (1, 2, 3):
+        for h in range(heads):
+            for t in range(4):
+                out_copies[h, t, r].wait_recv()
 
 
 def settle(*refs):
@@ -270,16 +285,19 @@
     cut = [a.reshape(1, halves // ctx, total // halves, wide) for a in args[6:10]]
     args = args[:4] + (args[4].T, args[5].T, *cut, args[10])
     vmem = pl.BlockSpec(memory_space=pltpu.VMEM)
-    smem = pl.BlockSpec(memory_space=pltpu.SMEM)
     hbm = pl.BlockSpec(memory_space=pl.ANY)
     dma = pltpu.SemaphoreType.DMA
     shapes = [(tokens + B, width)] + [(tokens, width)] * 3 + [(1, rows, wide)] * 4
     outs = pl.pallas_call(
         functools.partial(kernel, lax.axis_size("dp")),
         out_shape=tuple(pltpu.VMEM(s, BF16) for s in shapes),
-        in_specs=[hbm] * 4 + [smem] * 2 + [hbm] * 4 + [smem],
+        in_specs=[hbm] * 11,
         out_specs=(vmem,) * 8,
         scratch_shapes=[
+            pltpu.SMEM(args[4].shape, jnp.int32),
+            pltpu.SMEM(args[5].shape, jnp.int32),
+            pltpu.SMEM(args[10].shape, jnp.int32),
+            pltpu.VMEM((4,) + cut[0].shape, BF16),
             pltpu.VMEM((4, tokens, width), BF16),
             pltpu.VMEM((4, halves, total // halves, D), BF16),
             pltpu.VMEM((4, halves, total // halves, D), BF16),
@@ -291,6 +309,8 @@
             pltpu.VMEM((total, total), BF16),
             pltpu.VMEM((total, total), BF16),
             pltpu.VMEM((B, width), BF16),
+            dma((3,)),
+            dma((4,)),
             dma((4,)),
             dma((heads, 4)),
             dma((heads, 4, 3)),

time: 32.8 us -> 31.8 us (0.970)
  Pallas kernels: 32 us -> 31.1 us
    pallas_call x1, Pallas kernels: 30.5 us -> 29.5 us  [shards(): pl.pallas_call(functools.partial(kernel, lax.axis_size('dp')), out_shape=...]
where the time goes in v2:
time: 31.8 us; the launch traced here: 31.7 us
  Pallas kernels  31.1 us (98%)
  between operations  0.65 us (2%)
    pallas_call x1, Pallas kernels, shards(): pl.pallas_call(functools.partial(kernel, lax.axis_size('dp')), out_shape=...  29.5 us
    pallas_call x1, Pallas kernels, shards(): pl.pallas_call(settle, out_shape=tuple((jax.ShapeDtypeStruct(s, BF16) for...  1.57 us

profile of v2, /device:TPU:1, one launch (start us, length us, event | category | flops | bytes accessed | tf_op | source)
XLA Modules:
  0.0 31.7 jit_solution(13577077766809628238)
XLA Ops:
  0.6 29.5 %attention.1 = (bf16[896,256]{1,0:T(8,128)(2,1)S(1)}, bf16[768,256]{1,0:T(8,128)(2,1)S(1)}, bf16[768,256]{1,0:T(8,128)(2,1)S(1)}, bf16[768,256]{1,0:T(8,128)(2,1...) custom-call(bf16[768,256]{1,0:T(8,128)(2,1)} %qs_hbm.1, ...), custom_call_target="tpu_custom_call" | custom-call | tf_op jit(solution)/shard_map/attention/pallas_call | solution.py:291
  30.2 1.6 %settle.1 = (bf16[896,256]{1,0:T(8,128)(2,1)}, bf16[768,256]{1,0:T(8,128)(2,1)}, bf16[768,256]{1,0:T(8,128)(2,1)}, bf16[768,256]{1,0:T(8,128)(2,1)}, bf16[1,128,...) custom-call(bf16[896,256]{1,0:T(8,128)(2,1)S(1)} %get-tuple-element., ...), custom_call_target="tpu_custom_call" | custom-call | tf_op jit(solution)/shard_map/settle/pallas_call | solution.py:326

commit v3 on v2

--- a/solution.py
+++ b/solution.py
@@ -11,6 +11,7 @@
 D = 128
 B = 128
 NEG = -1e30
+LEADER = 1
 SCALE = D**-0.5
 EXP_SCALE = SCALE * math.log2(math.e)
 MESH = pl.DeviceIdType.MESH
@@ -50,6 +51,7 @@
     os_ref, dqs_ref, dks_ref, dvs_ref, ol_ref, dql_ref, dkl_ref, dvl_ref,
     len_ref, dest_ref, order_ref, staged, short, arrived0, arrived1, placed, result, leaving, w_band, g_band, w_long, g_long, moved,
     int_sem, stage_sem, short_sem, own_sem, in_send, in_recv, out_send, out_recv, move_send, move_recv,
+    cross_sem, go_sem,
 ):
     dp = lax.axis_index("dp")
     me = lax.axis_index("ctx")
@@ -93,12 +95,21 @@
     barrier = pltpu.get_barrier_semaphore()
     for peer in peers.values():
         pl.semaphore_signal(barrier, inc=1, device_id=(dp, peer), device_id_type=MESH)
-    pl.semaphore_signal(barrier, inc=1, device_id=(partner, me), device_id_type=MESH)
+
+    @pl.when(me == LEADER)
+    def _():
+        pl.semaphore_signal(barrier, inc=1, device_id=(partner, me), device_id_type=MESH)
+
     for copy in stage_copies + int_copies + own_copies + short_copies:
         copy.start()
     for copy in stage_copies:
         copy.wait()
-    pl.semaphore_wait(barrier, 4)
+    pl.semaphore_wait(barrier, jnp.where(me == LEADER, 4, 3))
+
+    @pl.when(me == LEADER)
+    def _():
+        pl.semaphore_signal(cross_sem, inc=1, device_id=(partner, me), device_id_type=MESH)
+
 
     in_copies = {}
     for h in range(heads):
@@ -178,14 +189,27 @@
         device_id=(partner, me),
         device_id_type=MESH,
     )
-    move.start()
     keep = jnp.concatenate([row, row], axis=1) < B - tail_moved
     os_ref[here, :] = jnp.where(keep, attended.astype(F32), 0.0).astype(BF16)
     for n in range(blocks - 2, -1, -1):
         here, attended = short_block(n)
         os_ref[here, :] = attended
         short_keys(n + 1)
+        if n == blocks // 2:
+
+            @pl.when(me == LEADER)
+            def _():
+                pl.semaphore_wait(cross_sem, 1)
+                for peer in peers.values():
+                    pl.semaphore_signal(go_sem, inc=1, device_id=(dp, peer), device_id_type=MESH)
+
     short_keys(0)
+
+    @pl.when(me != LEADER)
+    def _():
+        pl.semaphore_wait(go_sem, 1)
+
+    move.start()
 
     order = [order_ref[i] for i in range(halves)]
     found = []
@@ -319,6 +343,8 @@
             dma((heads, 4, 3)),
             dma,
             dma,
+            pltpu.SemaphoreType.REGULAR,
+            pltpu.SemaphoreType.REGULAR,
         ],
         compiler_params=pltpu.CompilerParams(collective_id=0, has_side_effects=True),
         name="attention",

time: 31.8 us -> 31.6 us (level)
  no operation moved by 1% of the time
where the time goes in v3:
time: 31.6 us; the launch traced here: 31.5 us
  Pallas kernels  30.9 us (98%)
  between operations  0.65 us (2%)
    pallas_call x1, Pallas kernels, shards(): pl.pallas_call(functools.partial(kernel, lax.axis_size('dp')), out_shape=...  29.3 us
    pallas_call x1, Pallas kernels, shards(): pl.pallas_call(settle, out_shape=tuple((jax.ShapeDtypeStruct(s, BF16) for...  1.57 us

profile of v3, /device:TPU:1, one launch (start us, length us, event | category | flops | bytes accessed | tf_op | source)
XLA Modules:
  0.0 31.5 jit_solution(8451147943450365417)
XLA Ops:
  0.6 29.3 %attention.1 = (bf16[896,256]{1,0:T(8,128)(2,1)S(1)}, bf16[768,256]{1,0:T(8,128)(2,1)S(1)}, bf16[768,256]{1,0:T(8,128)(2,1)S(1)}, bf16[768,256]{1,0:T(8,128)(2,1...) custom-call(bf16[768,256]{1,0:T(8,128)(2,1)} %qs_hbm.1, ...), custom_call_target="tpu_custom_call" | custom-call | tf_op jit(solution)/shard_map/attention/pallas_call | solution.py:315
  29.9 1.6 %settle.1 = (bf16[896,256]{1,0:T(8,128)(2,1)}, bf16[768,256]{1,0:T(8,128)(2,1)}, bf16[768,256]{1,0:T(8,128)(2,1)}, bf16[768,256]{1,0:T(8,128)(2,1)}, bf16[1,128,...) custom-call(bf16[896,256]{1,0:T(8,128)(2,1)S(1)} %get-tuple-element., ...), custom_call_target="tpu_custom_call" | custom-call | tf_op jit(solution)/shard_map/settle/pallas_call | solution.py:352

commit v4 on v2

--- a/solution.py
+++ b/solution.py
@@ -11,6 +11,8 @@
 D = 128
 B = 128
 NEG = -1e30
+LEADER = 2
+EARLY = 1
 SCALE = D**-0.5
 EXP_SCALE = SCALE * math.log2(math.e)
 MESH = pl.DeviceIdType.MESH
@@ -50,6 +52,7 @@
     os_ref, dqs_ref, dks_ref, dvs_ref, ol_ref, dql_ref, dkl_ref, dvl_ref,
     len_ref, dest_ref, order_ref, staged, short, arrived0, arrived1, placed, result, leaving, w_band, g_band, w_long, g_long, moved,
     int_sem, stage_sem, short_sem, own_sem, in_send, in_recv, out_send, out_recv, move_send, move_recv,
+    cross_sem, go_sem, in0_sem, in2_sem, all_sem,
 ):
     dp = lax.axis_index("dp")
     me = lax.axis_index("ctx")
@@ -90,31 +93,92 @@
                 )
             )
 
+    def tell(sem, *cores, rank=dp):
+        for core in cores:
+            pl.semaphore_signal(sem, inc=1, device_id=(rank, core), device_id_type=MESH)
+
     barrier = pltpu.get_barrier_semaphore()
-    for peer in peers.values():
-        pl.semaphore_signal(barrier, inc=1, device_id=(dp, peer), device_id_type=MESH)
-    pl.semaphore_signal(barrier, inc=1, device_id=(partner, me), device_id_type=MESH)
+
+    @pl.when(me == 1)
+    def _():
+        tell(barrier, 0, 2, 3)
+
+    @pl.when(me == 2)
+    def _():
+        tell(barrier, 3)
+        tell(barrier, 2, rank=partner)
+
+    @pl.when(me == 3)
+    def _():
+        tell(barrier, 1)
+
     for copy in stage_copies + int_copies + own_copies + short_copies:
         copy.start()
     for copy in stage_copies:
         copy.wait()
-    pl.semaphore_wait(barrier, 4)
-
-    in_copies = {}
-    for h in range(heads):
-        for r, peer in peers.items():
-            for t in range(4):
-                cols = pl.ds(pl.multiple_of(peer * heads * D + h * D, D), D)
-                copy = pltpu.make_async_remote_copy(
-                    src_ref=staged.at[t, 0, :, :, cols],
-                    dst_ref=arrived[h].at[t, pl.ds(me * mine, mine), :, :],
-                    send_sem=in_send.at[h, t, r - 1],
-                    recv_sem=in_recv.at[h, t, r - 1],
-                    device_id=(dp, peer),
-                    device_id_type=MESH,
-                )
-                copy.start()
-                in_copies[h, t, r] = copy
+    pl.semaphore_wait(barrier, 1 + me // 2)
+
+    @pl.when(me == 0)
+    def _():
+        tell(in0_sem, 1)
+        pl.semaphore_wait(all_sem, 1)
+
+    @pl.when(me == 3)
+    def _():
+        tell(in2_sem, 1)
+
+    def inbound(h, t, r, peer):
+        cols = pl.ds(pl.multiple_of(peer * heads * D + h * D, D), D)
+        return pltpu.make_async_remote_copy(
+            src_ref=staged.at[t, 0, :, :, cols],
+            dst_ref=arrived[h].at[t, pl.ds(me * mine, mine), :, :],
+            send_sem=in_send.at[h, t, r - 1],
+            recv_sem=in_recv.at[h, t, r - 1],
+            device_id=(dp, peer),
+            device_id_type=MESH,
+        )
+
+    def send(h, r, peer):
+        for t in range(4):
+            inbound(h, t, r, peer).start()
+
+    odd = lax.rem(me, 2)
+    first, second = 3 - odd, 2 + odd
+    first_peer = 3 - 2 * (me // 2)
+    second_peer = first_peer - 1
+
+    send(0, first, first_peer)
+
+    @pl.when(me == 1)
+    def _():
+        pl.semaphore_wait(in2_sem, 1)
+
+    @pl.when(me >= 2)
+    def _():
+        pl.semaphore_wait(all_sem, 1)
+
+    send(0, second, second_peer)
+
+    @pl.when(me == 1)
+    def _():
+        pl.semaphore_wait(in0_sem, 1)
+        tell(all_sem, 0, 2, 3)
+
+    @pl.when(me == LEADER)
+    def _():
+        tell(cross_sem, LEADER, rank=partner)
+
+    send(0, 1, peers[1])
+    for h in range(1, heads):
+        send(h, first, first_peer)
+        send(h, second, second_peer)
+        send(h, 1, peers[1])
+    in_copies = {
+        (h, t, r): inbound(h, t, r, peer)
+        for h in range(heads)
+        for r, peer in peers.items()
+        for t in range(4)
+    }
     for copy in int_copies + short_copies:
         copy.wait()
 
@@ -178,15 +242,8 @@
         device_id=(partner, me),
         device_id_type=MESH,
     )
-    move.start()
     keep = jnp.concatenate([row, row], axis=1) < B - tail_moved
     os_ref[here, :] = jnp.where(keep, attended.astype(F32), 0.0).astype(BF16)
-    for n in range(blocks - 2, -1, -1):
-        here, attended = short_block(n)
-        os_ref[here, :] = attended
-        short_keys(n + 1)
-    short_keys(0)
-
     order = [order_ref[i] for i in range(halves)]
     found = []
     for p in range(halves):
@@ -195,13 +252,23 @@
             at = jnp.where(order[i] == p, i, at)
         found.append(at)
     lower = col <= row
-    out_copies = {}
+
+    def outbound(h, t, r, peer):
+        cols = pl.ds(pl.multiple_of(me * heads * D + h * D, D), D)
+        return pltpu.make_async_remote_copy(
+            src_ref=leaving.at[h, t, pl.ds(pl.multiple_of(peer * rows, rows), rows), :],
+            dst_ref=long_outs[t].at[0, :, cols],
+            send_sem=out_send.at[h, t, r - 1],
+            recv_sem=out_recv.at[h, t, r - 1],
+            device_id=(dp, peer),
+            device_id_type=MESH,
+        )
 
     def store(t, n, value):
         for i in range(B // half):
             result[t, n * (B // half) + i] = value[i * half : (i + 1) * half]
 
-    for h in range(heads):
+    def long_pass(h):
         for t in range(4):
             own_copies[h * 4 + t].wait()
         for r in peers:
@@ -234,24 +301,45 @@
             for i in range(halves):
                 leaving[h, t, i * half : (i + 1) * half, :] = result[t, order[i]]
         cols = pl.ds(pl.multiple_of(me * heads * D + h * D, D), D)
-        for r, peer in peers.items():
+        for r, peer in ((first, first_peer), (second, second_peer), (1, peers[1])):
             for t in range(4):
-                copy = pltpu.make_async_remote_copy(
-                    src_ref=leaving.at[h, t, pl.ds(pl.multiple_of(peer * rows, rows), rows), :],
-                    dst_ref=long_outs[t].at[0, :, cols],
-                    send_sem=out_send.at[h, t, r - 1],
-                    recv_sem=out_recv.at[h, t, r - 1],
-                    device_id=(dp, peer),
-                    device_id_type=MESH,
-                )
-                copy.start()
-                out_copies[h, t, r] = copy
+                outbound(h, t, r, peer).start()
         for t in range(4):
             long_outs[t][0, :, cols] = leaving[h, t, pl.ds(pl.multiple_of(me * rows, rows), rows), :]
+
+    for n in range(blocks - 2, -1, -1):
+        here, attended = short_block(n)
+        os_ref[here, :] = attended
+        short_keys(n + 1)
+        if n == EARLY:
+            long_pass(0)
+        if n == blocks // 2:
+
+            @pl.when(me == LEADER)
+            def _():
+                pl.semaphore_wait(cross_sem, 1)
+                tell(go_sem, 0, 1, 3)
+
+    short_keys(0)
+
+    @pl.when(me != LEADER)
+    def _():
+        pl.semaphore_wait(go_sem, 1)
+
+    move.start()
+    for h in range(1, heads):
+        long_pass(h)
+
 
     for copy in in_copies.values():
         copy.wait_send()
     move.wait()
+    out_copies = {
+        (h, t, r): outbound(h, t, r, peer)
+        for h in range(heads)
+        for r, peer in peers.items()
+        for t in range(4)
+    }
     for r in (1, 2, 3):
         for h in range(heads):
             for t in range(4):
@@ -319,6 +407,11 @@
             dma((heads, 4, 3)),
             dma,
             dma,
+            pltpu.SemaphoreType.REGULAR,
+            pltpu.SemaphoreType.REGULAR,
+            pltpu.SemaphoreType.REGULAR,
+            pltpu.SemaphoreType.REGULAR,
+            pltpu.SemaphoreType.REGULAR,
         ],
         compiler_params=pltpu.CompilerParams(collective_id=0, has_side_effects=True),
         name="attention",

time: 31.8 us -> 30.1 us (0.947)
  Pallas kernels: 31.1 us -> 29.2 us
    pallas_call x1, Pallas kernels: 29.5 us -> 27.7 us  [shards(): pl.pallas_call(functools.partial(kernel, lax.axis_size('dp')), out_shape=...]
where the time goes in v4:
time: 30.1 us; the launch traced here: 29.9 us
  Pallas kernels  29.2 us (97%)
  between operations  0.65 us (2%)
    pallas_call x1, Pallas kernels, shards(): pl.pallas_call(functools.partial(kernel, lax.axis_size('dp')), out_shape=...  27.7 us
    pallas_call x1, Pallas kernels, shards(): pl.pallas_call(settle, out_shape=tuple((jax.ShapeDtypeStruct(s, BF16) for...  1.57 us

profile of v4, /device:TPU:1, one launch (start us, length us, event | category | flops | bytes accessed | tf_op | source)
XLA Modules:
  0.0 29.9 jit_solution(17317788323405175086)
XLA Ops:
  0.6 27.7 %attention.1 = (bf16[896,256]{1,0:T(8,128)(2,1)S(1)}, bf16[768,256]{1,0:T(8,128)(2,1)S(1)}, bf16[768,256]{1,0:T(8,128)(2,1)S(1)}, bf16[768,256]{1,0:T(8,128)(2,1...) custom-call(bf16[768,256]{1,0:T(8,128)(2,1)} %qs_hbm.1, ...), custom_call_target="tpu_custom_call" | custom-call | tf_op jit(solution)/shard_map/attention/pallas_call | solution.py:379
  28.3 1.6 %settle.1 = (bf16[896,256]{1,0:T(8,128)(2,1)}, bf16[768,256]{1,0:T(8,128)(2,1)}, bf16[768,256]{1,0:T(8,128)(2,1)}, bf16[768,256]{1,0:T(8,128)(2,1)}, bf16[1,128,...) custom-call(bf16[896,256]{1,0:T(8,128)(2,1)S(1)} %get-tuple-element., ...), custom_call_target="tpu_custom_call" | custom-call | tf_op jit(solution)/shard_map/settle/pallas_call | solution.py:419

commit v5 on v4

--- a/solution.py
+++ b/solution.py
@@ -168,10 +168,10 @@
     def _():
         tell(cross_sem, LEADER, rank=partner)
 
-    send(0, 1, peers[1])
     for h in range(1, heads):
         send(h, first, first_peer)
         send(h, second, second_peer)
+    for h in range(heads):
         send(h, 1, peers[1])
     in_copies = {
         (h, t, r): inbound(h, t, r, peer)

time: 30.1 us -> 29.9 us (level)
  no operation moved by 1% of the time
where the time goes in v5:
time: 29.9 us; the launch traced here: 29.8 us
  Pallas kernels  29.1 us (97%)
  between operations  0.65 us (2%)
    pallas_call x1, Pallas kernels, shards(): pl.pallas_call(functools.partial(kernel, lax.axis_size('dp')), out_shape=...  27.6 us
    pallas_call x1, Pallas kernels, shards(): pl.pallas_call(settle, out_shape=tuple((jax.ShapeDtypeStruct(s, BF16) for...  1.57 us

profile of v5, /device:TPU:1, one launch (start us, length us, event | category | flops | bytes accessed | tf_op | source)
XLA Modules:
  0.0 29.8 jit_solution(14908466208567309134)
XLA Ops:
  0.6 27.6 %attention.1 = (bf16[896,256]{1,0:T(8,128)(2,1)S(1)}, bf16[768,256]{1,0:T(8,128)(2,1)S(1)}, bf16[768,256]{1,0:T(8,128)(2,1)S(1)}, bf16[768,256]{1,0:T(8,128)(2,1...) custom-call(bf16[768,256]{1,0:T(8,128)(2,1)} %qs_hbm.1, ...), custom_call_target="tpu_custom_call" | custom-call | tf_op jit(solution)/shard_map/attention/pallas_call | solution.py:379
  28.2 1.6 %settle.1 = (bf16[896,256]{1,0:T(8,128)(2,1)}, bf16[768,256]{1,0:T(8,128)(2,1)}, bf16[768,256]{1,0:T(8,128)(2,1)}, bf16[768,256]{1,0:T(8,128)(2,1)}, bf16[1,128,...) custom-call(bf16[896,256]{1,0:T(8,128)(2,1)S(1)} %get-tuple-element., ...), custom_call_target="tpu_custom_call" | custom-call | tf_op jit(solution)/shard_map/settle/pallas_call | solution.py:419
